TPU v7x, 32 devices: a whole 2x2x4 slice. The times are simulated.
32 devices in a mesh: ha: 8 (over z, core), wa: 2 (over y), ba: 2 (over x).
Axes of the slice: x: 2, y: 2, z: 4, core: 2. Of those that a mesh axis runs over, the one named last changes fastest.
Arguments:
- tokens: bfloat16 [2, 128, 64, 384], P('ba', 'ha', 'wa'), may hold values from -6 to 6
- cotangent: bfloat16 [2, 128, 64, 384], P('ba', 'ha', 'wa'), may hold values from -6 to 6
- w_qkv: bfloat16 [384, 1152], replicated, may hold values from -0.20412415 to 0.20412415
- w_proj: bfloat16 [384, 384], replicated, may hold values from -0.3125 to 0.3125
- table_logits: float32 [12, 225], replicated, may hold values from -6 to 6
- logit_scale: float32 [12], replicated, may hold values from 1 to 5.5
- gain: float32 [384], replicated, may hold values from 0.5 to 1.5
Outputs:
- d_tokens: bfloat16 [2, 128, 64, 384], P('ba', 'ha', 'wa')
- d_wqkv: float32 [384, 1152], P(None, 'ba')
- d_wproj: float32 [384, 384], P(None, 'ba')
- d_table: float32 [12, 225], replicated
- d_scale: float32 [12], replicated
- d_gain: float32 [384], replicated
All inputs are finite; a program needn't handle non-finite values.
Results may differ from a plain program's by a relative error of at most 0.01.
The roundings to bfloat16 on the way count: a program that leaves them out, or rounds other values in their place, can miss the bound.
Values may be sent and summed in bfloat16 or wider, within the bound.
A program may use at most 64 MiB of HBM per device.

v0:
```python
import math
import jax
import jax.numpy as jnp
from jax import lax
from jax.sharding import PartitionSpec as P

WIN = 8
EPS_NORM = 1e-05
MASK_FILL = -100.0
SCALE_CAP = math.log(100.0)
BIAS_RANGE = 16.0
HIGHEST = lax.Precision.HIGHEST


def from_behind(block, axis, distance):
    devices = range(lax.axis_size(axis))
    route = [((i - distance) % len(devices), i) for i in devices]
    return lax.ppermute(block, axis, route)


def coarse_product(form, left, right):
    return jnp.einsum(form, left, right, preferred_element_type=jnp.float32)


def fine_product(form, left, right):
    return jnp.einsum(form, left, right, precision=HIGHEST)


def to_windows(block, window):
    images, height, width, depth = block.shape
    tiles = block.reshape(images, height // window, window, width // window, window, depth)
    tiles = tiles.transpose(0, 1, 3, 2, 4, 5)
    return tiles.reshape(images, height // window * (width // window), window * window, depth)


def from_windows(tiles, images, height, width, window):
    depth = tiles.shape[-1]
    grid = tiles.reshape(images, height // window, width // window, window, window, depth)
    return grid.transpose(0, 1, 3, 2, 4, 5).reshape(images, height, width, depth)


def position_onehot(window):
    places = jnp.arange(window * window, dtype=jnp.int32)
    row_of = places // window
    col_of = places % window
    offset = (row_of[:, None] - row_of[None, :] + window - 1) * (2 * window - 1) + (
        col_of[:, None] - col_of[None, :] + window - 1
    )
    entries = jnp.arange((2 * window - 1) ** 2, dtype=jnp.int32)
    return (offset.reshape(-1)[:, None] == entries[None, :]).astype(jnp.float32)


def region_of(coords, extent, window):
    return (coords >= extent - window).astype(jnp.int32) + (coords >= extent - window // 2).astype(
        jnp.int32
    )


def region_mask(row_start, col_start, rows, cols, height, width, window):
    row_label = region_of(row_start + jnp.arange(rows, dtype=jnp.int32), height, window)
    col_label = region_of(col_start + jnp.arange(cols, dtype=jnp.int32), width, window)
    labels = row_label[:, None] * 3 + col_label[None, :]
    labels = labels.reshape(rows // window, window, cols // window, window).transpose(0, 2, 1, 3)
    labels = labels.reshape(-1, window * window)
    return jnp.where(labels[:, :, None] != labels[:, None, :], MASK_FILL, 0.0).astype(jnp.float32)


def grads_region(block, grad_block, row_start, col_start, height, width, window, params):
    w_qkv, w_proj, table_logits, logit_scale, gain = params
    images, rows, cols, depth = block.shape
    heads = logit_scale.shape[0]
    head_dim = depth // heads
    tiles = to_windows(block, window)
    grad_tiles = to_windows(grad_block, window)
    count = tiles.shape[1]
    length = window * window
    flat = tiles.reshape(-1, depth)
    qkv = jnp.dot(flat, w_qkv, preferred_element_type=jnp.float32).astype(jnp.bfloat16)
    qkv = qkv.reshape(images, count, length, 3, heads, head_dim)
    query = qkv[:, :, :, 0].astype(jnp.float32)
    keys = qkv[:, :, :, 1].astype(jnp.float32)
    values = qkv[:, :, :, 2]
    query_inv = lax.rsqrt(jnp.sum(query * query, -1, keepdims=True) + 1.0)
    key_inv = lax.rsqrt(jnp.sum(keys * keys, -1, keepdims=True) + 1.0)
    unit_query = query * query_inv
    unit_key = keys * key_inv
    scale = jnp.exp(jnp.minimum(logit_scale, SCALE_CAP))
    onehot = position_onehot(window)
    sigma = jax.nn.sigmoid(table_logits)
    rel_bias = jnp.dot(sigma * BIAS_RANGE, onehot.T, precision=HIGHEST).reshape(
        heads, length, length
    )
    mask = region_mask(row_start, col_start, rows, cols, height, width, window)
    cosine = fine_product("bnqhd,bnkhd->bnhqk", unit_query, unit_key)
    scores = scale[:, None, None] * cosine + rel_bias[None, None] + mask[None, :, None]
    top = jnp.max(scores, -1, keepdims=True)
    expo = jnp.exp(scores - top)
    probs = expo / jnp.sum(expo, -1, keepdims=True)
    probs_low = probs.astype(jnp.bfloat16)
    attended = (
        coarse_product("bnhqk,bnkhd->bnqhd", probs_low, values)
        .astype(jnp.bfloat16)
        .reshape(-1, depth)
    )
    proj = jnp.dot(attended, w_proj, preferred_element_type=jnp.float32)
    centre = proj - jnp.mean(proj, -1, keepdims=True)
    inv_std = lax.rsqrt(jnp.mean(centre * centre, -1, keepdims=True) + EPS_NORM)
    normed = centre * inv_std
    upstream = grad_tiles.reshape(-1, depth).astype(jnp.float32)
    d_gain = jnp.sum(upstream * normed, 0)
    scaled = upstream * gain
    d_proj = inv_std * (
        scaled
        - jnp.mean(scaled, -1, keepdims=True)
        - normed * jnp.mean(scaled * normed, -1, keepdims=True)
    )
    d_proj = d_proj.astype(jnp.bfloat16)
    d_wproj = jnp.dot(attended.T, d_proj, preferred_element_type=jnp.float32)
    d_att = jnp.dot(d_proj, w_proj.T, preferred_element_type=jnp.float32).astype(jnp.bfloat16)
    d_att = d_att.reshape(images, count, length, heads, head_dim)
    d_probs = coarse_product("bnqhd,bnkhd->bnhqk", d_att, values)
    d_values = coarse_product("bnhqk,bnqhd->bnkhd", probs_low, d_att)
    d_scores = probs * (d_probs - jnp.sum(d_probs * probs, -1, keepdims=True))
    d_bias = jnp.sum(d_scores, (0, 1)).reshape(heads, length * length)
    d_table = jnp.dot(d_bias, onehot, precision=HIGHEST) * (BIAS_RANGE * sigma * (1.0 - sigma))
    live = (logit_scale < SCALE_CAP).astype(jnp.float32)
    d_scale = jnp.sum(d_scores * cosine, (0, 1, 3, 4)) * scale * live
    d_cos = d_scores * scale[:, None, None]
    d_unit_q = fine_product("bnhqk,bnkhd->bnqhd", d_cos, unit_key)
    d_unit_k = fine_product("bnhqk,bnqhd->bnkhd", d_cos, unit_query)
    d_query = query_inv * (
        d_unit_q - unit_query * jnp.sum(unit_query * d_unit_q, -1, keepdims=True)
    )
    d_key = key_inv * (d_unit_k - unit_key * jnp.sum(unit_key * d_unit_k, -1, keepdims=True))
    d_qkv = jnp.stack([d_query, d_key, d_values], 3).astype(jnp.bfloat16).reshape(-1, 3 * depth)
    d_wqkv = jnp.dot(flat.T, d_qkv, preferred_element_type=jnp.float32)
    d_flat = jnp.dot(d_qkv, w_qkv.T, preferred_element_type=jnp.float32).astype(jnp.bfloat16)
    d_block = from_windows(d_flat.reshape(images, count, length, depth), images, rows, cols, window)
    return (d_block, (d_wqkv, d_wproj, d_table, d_scale, d_gain))


def shift_in(tokens, cotangent, shift):
    stacked = jnp.stack([tokens, cotangent])
    below = from_behind(stacked[:, :, :shift], "ha", -1)
    tall = jnp.concatenate([stacked[:, :, shift:], below], 2)
    beside = from_behind(tall[:, :, :, :shift], "wa", -1)
    moved = jnp.concatenate([tall[:, :, :, shift:], beside], 3)
    return (moved[0], moved[1])


def shift_out(grads, shift):
    rows = grads.shape[1]
    cols = grads.shape[2]
    right = from_behind(grads[:, :, cols - shift :], "wa", 1)
    wide = jnp.concatenate([right, grads[:, :, : cols - shift]], 2)
    lower = from_behind(wide[:, rows - shift :], "ha", 1)
    return jnp.concatenate([lower, wide[:, : rows - shift]], 1)


def shards(tokens, cotangent, w_qkv, w_proj, table_logits, logit_scale, gain):
    rows = tokens.shape[1]
    cols = tokens.shape[2]
    shift = WIN // 2
    height = rows * lax.axis_size("ha")
    width = cols * lax.axis_size("wa")
    row_base = lax.axis_index("ha") * rows
    col_base = lax.axis_index("wa") * cols
    params = (w_qkv, w_proj, table_logits, logit_scale, gain)
    moved, moved_grad = shift_in(tokens, cotangent, shift)
    d_moved, parts = grads_region(moved, moved_grad, row_base, col_base, height, width, WIN, params)
    back = shift_out(d_moved, shift)
    d_tokens = (cotangent.astype(jnp.float32) + back.astype(jnp.float32)).astype(jnp.bfloat16)
    d_wqkv, d_wproj, d_table, d_scale, d_gain = parts
    half_qkv, half_proj = (
        lax.psum_scatter(d_wqkv.astype(jnp.bfloat16), "ba", scatter_dimension=1, tiled=True).astype(
            jnp.float32
        ),
        lax.psum_scatter(
            d_wproj.astype(jnp.bfloat16), "ba", scatter_dimension=1, tiled=True
        ).astype(jnp.float32),
    )
    half_qkv, half_proj = lax.psum((half_qkv, half_proj), ("ha", "wa"))
    d_table, d_scale, d_gain = lax.psum((d_table, d_scale, d_gain), ("ha", "wa", "ba"))
    return (d_tokens, half_qkv, half_proj, d_table, d_scale, d_gain)


def solution(mesh):
    return jax.shard_map(
        shards,
        mesh=mesh,
        in_specs=(P("ba", "ha", "wa", None), P("ba", "ha", "wa", None), P(), P(), P(), P(), P()),
        out_specs=(P("ba", "ha", "wa", None), P(None, "ba"), P(None, "ba"), P(), P(), P()),
        check_vma=False,
    )
```

profile of v0, /device:TPU:0, one launch (start us, length us, event | category | flops | bytes accessed | tf_op | source)
XLA Modules:
  0.0 213.7 jit_solution(15621993046436900654)
XLA Ops:
  7.2 1.0 pad_maximum_fusion.2
  8.3 4.6 %collective-permute-start = (bf16[2,1,4,32,384]{4,3,2,1,0:T(8,128)(2,1)S(1)}, bf16[2,1,4,32,384]{4,3,2,1,0:T(8,128)(2,1)S(1)}, u32[]{:S(2)}, u32[]{:S(2)}) collective-permute-start(bf16[2,1,4,32,384]{4,3,2,1,0:T(8,128)(2,1)S(1)} %pad_maximum_fusion.2), channel_id=1, source_target_pairs={{4,0},{8,4},{12,8},{16,12},{20,16},{24,20},{28,24},{0,28},{5,1},{9... | collective-permute-start | bytes 589832 | tf_op jit(solution)/shard_map/ppermute | solution.py:18
  12.8 1.1 fusion.52
  14.2 0.8 compare_select_fusion
  15.2 2.0 fusion.2
  17.4 0.9 copy.85
  18.3 1.6 collective-permute-start.1
  20.2 2.8 %collective-permute-done.1 = bf16[2,1,16,4,384]{4,3,2,1,0:T(4,128)(2,1)S(1)} collective-permute-done((bf16[2,1,16,4,384]{4,3,2,1,0:T(4,128)(2,1)S(1)}, bf16[2,1,16,4,384]{4,3,2,1,0:T(4,128)(2,1)S(1)}, u32[]{:S(2)}, u32[]{:S(2)}) %collective-permute-start.1) | collective-permute-done | bytes 98336 | tf_op jit(solution)/shard_map/ppermute | solution.py:18
  23.0 0.9 fusion.57
  24.0 0.7 copy-done.9
  24.7 0.8 convolution_convert_fusion
  25.5 0.6 copy.82
  26.1 3.0 %reshape.449 = bf16[1,8,64,3,12,32]{2,1,5,4,3,0:T(8,128)(2,1)} reshape(bf16[512,1152]{0,1:T(8,128)(2,1)S(1)} %copy.82) | data formatting | bytes 2359296 | tf_op jit(solution)/shard_map/reshape | solution.py:79
  29.2 1.8 fusion.67
  31.7 5.2 %fusion.29 = f32[8,12,64,64]{2,3,1,0:T(8,128)S(1)} fusion(f32[8,64,12]{1,2,0:T(8,128)S(1)} %add_rsqrt_fusion.1, f32[8,64,12]{1,2,0:T(8,128)S(1)} %add_rsqrt_fusion, bf16[1,8,64,1,12,32]{2,1,5,4,3,0:T(8,128)(2,1)S(1)} %get-tuple-element.16, bf16[1,8,64,1,12,32]{2,1,5,4,3,0:T(8,128)(2,1)S(1)} %get-tuple-element.17), kind=kOutput, calls=%fused_computation.41 | convolution fusion | flops 151781376 | bytes 2408448 | tf_op jit(solution)/shard_map/bnqhd,bnkhd->bnhqk/dot_general | solution.py:26
  36.9 1.2 fusion.68
  38.2 0.5 copy-done.1
  38.6 0.5 fusion.40
  39.2 1.1 copy-done.3
  40.3 0.5 copy.88
  40.8 1.3 reshape.451
  42.1 1.6 fusion.69
  43.9 0.9 copy.89
  44.8 2.3 %copy.90 = f32[512,384]{0,1:T(8,128)} copy(f32[512,384]{1,0:T(8,128)} %bitcast.140) | data formatting | bytes 1572864 | tf_op jit(solution)/shard_map/convert_element_type | solution.py:109
  47.1 1.2 fusion.42
  48.3 1.4 multiply_reduce_fusion.2
  49.8 1.4 multiply_convert_fusion
  51.7 1.1 convolution_convert_fusion.5
  53.0 1.3 reshape.452
  54.3 3.6 %multiply_reduce_fusion.1 = (f32[8,12,64]{2,1,0:T(8,128)S(1)}, f32[8,12,64,64]{2,3,1,0:T(8,128)S(1)}) fusion(f32[8,12,64,64]{2,3,1,0:T(8,128)} %copy-done.3, f32[8,12,64]{2,1,0:T(8,128)S(1)} %get-tuple-element.21, bf16[1,8,64,1,12,32]{2,1,5,4,3,0:T(8,128)(2,1)} %copy-done.14, bf16[8,64,12,32]{1,0,3,2:T(8,128)(2,1)} %reshape.452), kind=kOutput, calls=%fused_computation.7 | convolution fusion | flops 26339328 | bytes 3981312 | tf_op jit(solution)/shard_map/bnqhd,bnkhd->bnhqk/dot_general | solution.py:22
  57.9 0.6 copy-done.4
  58.6 2.2 %multiply_reduce_fusion = (f32[12]{0:T(128)S(1)}, f32[12,64,64]{1,2,0:T(8,128)}, f32[8,12,64,64]{2,3,1,0:T(8,128)S(1)}) fusion(f32[8,12,64,64]{2,3,1,0:T(8,128)S(1)} %copy-done.2, f32[8,12,64,64]{2,3,1,0:T(8,128)S(1)} %get-tuple-element.26, f32[8,12,64]{2,1,0:T(8,128)S(1)} %get-tuple-element.25, f32[8,12,64,64]{2,3,1,0:T(8,128)S(1)} %copy-done.4, ...), kind=kLoop, calls=%fused_computation.5 | loop fusion | flops 2310132 | bytes 6537264 | tf_op jit(solution)/shard_map/reduce_sum | solution.py:127
  60.7 4.3 %fusion.22 = (f32[8,64,12]{1,2,0:T(8,128)S(1)}, f32[8,12,32,64]{3,2,1,0:T(8,128)}) fusion(f32[8,64,12]{1,2,0:T(8,128)S(1)} %add_rsqrt_fusion.1, bf16[1,8,64,1,12,32]{2,1,5,4,3,0:T(8,128)(2,1)S(1)} %get-tuple-element.17, f32[8,12,64,64]{2,3,1,0:T(8,128)S(1)} %get-tuple-element.15, f32[12]{0:T(128)S(1)} %minimum_exponential_fusion, ...), kind=kOutput, calls=%fused_computation.35 | convolution fusion | flops 152561664 | bytes 3219504 | tf_op jit(solution)/shard_map/bnhqk,bnkhd->bnqhd/dot_general | solution.py:26
  65.0 6.8 %fusion.18 = (f32[8,64,12]{1,2,0:T(8,128)}, f32[8,12,32,64]{3,2,1,0:T(8,128)}) fusion(f32[8,64,12]{1,2,0:T(8,128)S(1)} %add_rsqrt_fusion, bf16[1,8,64,1,12,32]{2,1,5,4,3,0:T(8,128)(2,1)S(1)} %get-tuple-element.16, f32[8,12,64,64]{2,3,1,0:T(8,128)S(1)} %get-tuple-element.15, f32[12]{0:T(128)S(1)} %minimum_exponential_fusion, ...), kind=kOutput, calls=%fused_computation.31 | convolution fusion | flops 152561664 | bytes 3219504 | tf_op jit(solution)/shard_map/bnhqk,bnqhd->bnkhd/dot_general | solution.py:26
  71.9 0.9 convolution_bitcast_fusion
  73.1 2.6 %fusion.21 = (bf16[1,8,64,1,12,32]{2,5,4,1,3,0:T(8,128)(2,1)S(1)}, bf16[1,8,64,1,12,32]{2,5,4,1,3,0:T(8,128)(2,1)S(1)}) fusion(f32[8,12,32,64]{3,2,1,0:T(8,128)} %get-tuple-element.28, f32[8,64,12]{1,2,0:T(8,128)} %get-tuple-element.27, f32[8,64,12]{1,2,0:T(8,128)S(1)} %add_rsqrt_fusion, bf16[1,8,64,1,12,32]{2,1,5,4,3,0:T(8,128)(2,1)S(1)} %get-tuple-element.16, ...), kind=kLoop, calls=%fused_computation.34 | loop fusion | flops 2359296 | bytes 3244032 | tf_op jit(solution)/shard_map/stack | solution.py:135
  75.7 0.6 maximum_convert_fusion
  76.3 2.7 %copy.98 = bf16[1,8,64,3,12,32]{2,1,5,4,3,0:T(8,128)(2,1)S(1)} copy(bf16[1,8,64,3,12,32]{2,5,4,1,3,0:T(8,128)(2,1)S(1)} %maximum_convert_fusion) | data formatting | bytes 2359296 | tf_op jit(solution)/shard_map/convert_element_type | solution.py:135
  79.1 2.4 %convert_element_type.207 = bf16[512,1152]{0,1:T(8,128)(2,1)} reshape(bf16[1,8,64,3,12,32]{2,1,5,4,3,0:T(8,128)(2,1)S(1)} %copy.98) | data formatting | bytes 2359296 | tf_op jit(solution)/shard_map/convert_element_type | solution.py:135
  81.5 3.1 %convolution_convert_fusion.1 = bf16[384,1152]{0,1:T(8,128)(2,1)} fusion(bf16[512,1152]{0,1:T(8,128)(2,1)} %convert_element_type.207, bf16[512,384]{1,0:T(8,128)(2,1)} %bitcast.142), kind=kOutput, calls=%fused_computation.15 | convolution fusion | flops 453427200 | bytes 2457600 | tf_op jit(solution)/shard_map/dot_general | solution.py:136
  84.9 0.9 copy-done.11
  85.8 0.9 convolution_convert_fusion.3
  86.8 1.6 collective-permute-start.2
  88.4 1.4 fusion.41
  89.8 1.1 collective-permute-done.2
  91.1 39.5 %all-reduce = (f32[12,225]{1,0:T(8,128)}, f32[12]{0:T(128)}, f32[384]{0:T(512)}) all-reduce(f32[12,225]{1,0:T(8,128)S(1)} %fusion.41, f32[12]{0:T(128)S(1)} %compare_select_fusion.1, f32[384]{0:T(512)S(1)} %get-tuple-element.8), channel_id=1, replica_groups=mesh['ha'=8,'wa'=2,'ba'=2] {'ha','wa','ba'}, use_global_device_ids=true, to_apply=%region_16.17 | all-reduce | flops 3096 | bytes 24768 | tf_op jit(solution)/shard_map/psum | solution.py:183
  130.6 0.9 add_convert_fusion
  131.5 75.2 %all-reduce.3 = (f32[384,576]{0,1:T(8,128)}, f32[384,192]{0,1:T(8,128)}) all-reduce(bf16[384,576]{0,1:T(8,128)(2,1)} %reduce-scatter.3.cloned.1.call-done, bf16[384,192]{0,1:T(8,128)(2,1)} %reduce-scatter.5.cloned.1.call-done), channel_id=1, replica_groups=mesh['ha'=8,'wa'=2,'ba'=2] {'ha','wa'}, use_global_device_ids=true, to_apply=%region_12.13 | all-reduce | flops 294912 | bytes 1769472 | tf_op jit(solution)/shard_map/psum | solution.py:182
  (75 shorter events, 3.4 us)
Async XLA Ops:
  7.2 17.5 %copy-start = (bf16[384,1152]{1,0:T(8,128)(2,1)S(1)}, bf16[384,1152]{1,0:T(8,128)(2,1)}, u32[]{:S(2)}) copy-start(bf16[384,1152]{1,0:T(8,128)(2,1)} %param.9) | copy-start | bytes 2654212
  7.2 8.0 %copy-start.17 = (f32[12,225]{1,0:T(8,128)S(1)}, f32[12,225]{1,0:T(8,128)}, u32[]{:S(2)}) copy-start(f32[12,225]{1,0:T(8,128)} %param.11) | copy-start | bytes 32404
  7.2 124.3 %reduce-scatter.5.cloned.1.call-start = ((), (), s32[]{:S(2)}) async-start(), calls=%async_computation.3 | async-start | bytes 442368 | tf_op jit(solution)/shard_map/reduce_scatter | solution.py:178
  8.3 10.0 %collective-permute-start = (bf16[2,1,4,32,384]{4,3,2,1,0:T(8,128)(2,1)S(1)}, bf16[2,1,4,32,384]{4,3,2,1,0:T(8,128)(2,1)S(1)}, u32[]{:S(2)}, u32[]{:S(2)}) collective-permute-start(bf16[2,1,4,32,384]{4,3,2,1,0:T(8,128)(2,1)S(1)} %pad_maximum_fusion.2), channel_id=1, source_target_pairs={{4,0},{8,4},{12,8},{16,12},{20,16},{24,20},{28,24},{0,28},{5,1},{9... | collective-permute-start | bytes 589832 | tf_op jit(solution)/shard_map/ppermute | solution.py:18
  14.0 4.3 %copy-start.18 = (f32[12]{0:T(128)S(1)}, f32[12]{0:T(128)}, u32[]{:S(2)}) copy-start(f32[12]{0:T(128)} %param.12) | copy-start | bytes 148
  18.3 4.7 %collective-permute-start.1 = (bf16[2,1,16,4,384]{4,3,2,1,0:T(4,128)(2,1)S(1)}, bf16[2,1,16,4,384]{4,3,2,1,0:T(4,128)(2,1)S(1)}, u32[]{:S(2)}, u32[]{:S(2)}) collective-permute-start(bf16[2,1,16,4,384]{4,3,2,1,0:T(4,128)(2,1)S(1)} %pad_maximum_fusion.4), channel_id=1, source_target_pairs={{2,0},{0,2},{3,1},{1,3},{6,4},{4,6},{7,5},{5,7},{10,8},{8,10},{11,... | collective-permute-start | bytes 294920 | tf_op jit(solution)/shard_map/ppermute | solution.py:18
  24.0 0.7 copy-start.9
  30.9 7.7 %copy-start.14 = (bf16[1,8,64,1,12,32]{2,1,5,4,3,0:T(8,128)(2,1)}, bf16[1,8,64,1,12,32]{2,1,5,4,3,0:T(8,128)(2,1)S(1)}, u32[]{:S(2)}) copy-start(bf16[1,8,64,1,12,32]{2,1,5,4,3,0:T(8,128)(2,1)S(1)} %get-tuple-element.18) | copy-start | bytes 1179652
  31.7 5.2 %copy-start.10 = (f32[12,64,64]{1,2,0:T(8,128)S(1)}, f32[12,64,64]{1,2,0:T(8,128)}, u32[]{:S(2)}) copy-start(f32[12,64,64]{1,2,0:T(8,128)} %copy.85) | copy-start | bytes 589828
  31.7 5.2 %copy-start.13 = (f32[8,64,64]{1,2,0:T(8,128)S(1)}, f32[8,64,64]{1,2,0:T(8,128)}, u32[]{:S(2)}) copy-start(f32[8,64,64]{1,2,0:T(8,128)} %compare_select_fusion) | copy-start | bytes 393220
  36.9 1.7 copy-start.1
  38.6 1.7 copy-start.3
  42.1 1.7 copy-start.6
  43.9 3.2 %copy-start.16 = (f32[384]{0:T(512)S(1)}, f32[384]{0:T(512)}, u32[]{:S(2)}) copy-start(f32[384]{0:T(512)} %param.13) | copy-start | bytes 4612
  49.8 1.4 copy-start.12
  49.8 1.9 copy-start.5
  54.3 3.6 %copy-start.2 = (f32[8,12,64,64]{2,3,1,0:T(8,128)S(1)}, f32[8,12,64,64]{2,3,1,0:T(8,128)}, u32[]{:S(2)}) copy-start(f32[8,12,64,64]{2,3,1,0:T(8,128)} %copy-done.1) | copy-start | bytes 4718596
  54.3 4.3 %copy-start.4 = (f32[8,12,64,64]{2,3,1,0:T(8,128)S(1)}, f32[8,12,64,64]{2,3,1,0:T(8,128)}, u32[]{:S(2)}) copy-start(f32[8,12,64,64]{2,3,1,0:T(8,128)} %copy-done.3) | copy-start | bytes 4718596
  65.0 6.8 %copy-start.15 = (bf16[8,64,12,32]{1,0,3,2:T(8,128)(2,1)S(1)}, bf16[8,64,12,32]{1,0,3,2:T(8,128)(2,1)}, u32[]{:S(2)}) copy-start(bf16[8,64,12,32]{1,0,3,2:T(8,128)(2,1)} %reshape.452) | copy-start | bytes 1179652
  72.8 58.7 %reduce-scatter.3.cloned.1.call-start = ((), (), s32[]{:S(2)}) async-start(), calls=%async_computation.2 | async-start | bytes 1327104 | tf_op jit(solution)/shard_map/reduce_scatter | solution.py:175
  81.5 3.1 %copy-start.8 = (f32[12,64,64]{1,2,0:T(8,128)S(1)}, f32[12,64,64]{1,2,0:T(8,128)}, u32[]{:S(2)}) copy-start(f32[12,64,64]{1,2,0:T(8,128)} %get-tuple-element.7) | copy-start | bytes 589828
  84.6 1.3 copy-start.11
  86.7 43.9 %copy-start.7 = (bf16[1,16,32,384]{3,2,1,0:T(8,128)(2,1)S(1)}, bf16[1,16,32,384]{3,2,1,0:T(8,128)(2,1)}, u32[]{:S(2)}) copy-start(bf16[1,16,32,384]{3,2,1,0:T(8,128)(2,1)} %param.8) | copy-start | bytes 1179652
  86.8 4.2 %collective-permute-start.2 = (bf16[1,16,4,384]{3,2,1,0:T(4,128)(2,1)S(1)}, bf16[1,16,4,384]{3,2,1,0:T(4,128)(2,1)S(1)}, u32[]{:S(2)}, u32[]{:S(2)}) collective-permute-start(bf16[1,16,4,384]{3,2,1,0:T(4,128)(2,1)S(1)} %slice.61), channel_id=1, source_target_pairs={{2,0},{0,2},{3,1},{1,3},{6,4},{4,6},{7,5},{5,7},{10,8},{8,10},{11,... | collective-permute-start | bytes 147464 | tf_op jit(solution)/shard_map/ppermute | solution.py:18
  91.0 39.6 %collective-permute-start.3 = (bf16[1,4,32,384]{3,2,1,0:T(8,128)(2,1)S(1)}, bf16[1,4,32,384]{3,2,1,0:T(8,128)(2,1)S(1)}, u32[]{:S(2)}, u32[]{:S(2)}) collective-permute-start(bf16[1,4,32,384]{3,2,1,0:T(8,128)(2,1)S(1)} %pad_maximum_fusion.3), channel_id=1, source_target_pairs={{28,0},{0,4},{4,8},{8,12},{12,16},{16,20},{20,24},{24,28},{29,1},{... | collective-permute-start | bytes 294920 | tf_op jit(solution)/shard_map/ppermute | solution.py:18
Sparse Core Ops, SparseCore 0:
  73.0 11.1 reduce-scatter.4
  87.0 19.1 reduce-scatter.2
where the time goes:
time: 218 us; the launch traced here: 214 us
  blocking collectives  115 us (53%)
  matrix products  32.7 us (15%)
  local copies, waits for them, and re-layouts  22.7 us (10%)
  other arithmetic  16.8 us (8%)
  between operations  14.7 us (7%)
  starting transfers between devices  8.08 us (4%)
  waiting for transfers between devices  4.03 us (2%)
    psum x1, blocking collectives, shards(): half_qkv, half_proj = lax.psum((half_qkv, half_proj), ('ha', 'wa'))  75.2 us
    psum x1, blocking collectives, shards(): lax.psum((d_table, d_scale, d_gain), ('ha', 'wa', 'ba'))  39.5 us
    dot_general x3, matrix products, fine_product(): return jnp.einsum(form, left, right, precision=HIGHEST)  16.3 us
    ppermute x4, starting transfers between devices, from_behind(): return lax.ppermute(block, axis, route)  7.79 us
    convert_element_type x2, local copies, waits for them, and re-layouts, grads_region(): jnp.stack([d_query, d_key, d_values], 3).astype(jnp.bfloat16)  5.15 us
    dot_general x3, matrix products, coarse_product(): return jnp.einsum(form, left, right, preferred_element_type=jnp.float32)  5.11 us
  transfers between devices with their start and end apart: 6, of which 2 were waited for; matrix products, arithmetic and copies ran while one was open for 10% of the time, Pallas kernels for 0%

commit v1 on v0

--- a/solution.py
+++ b/solution.py
@@ -1,3 +1,4 @@
+import functools
 import math
 import jax
 import jax.numpy as jnp
@@ -10,6 +11,14 @@
 SCALE_CAP = math.log(100.0)
 BIAS_RANGE = 16.0
 HIGHEST = lax.Precision.HIGHEST
+
+
+def test_files_on_mesh(q_in, across, a_name):
+    part_next = lax.psum(q_in, across)
+    return lax.psum(part_next, a_name)
+
+
+lead_desk_all = functools.partial(test_files_on_mesh, across="ha", a_name="wa")
 
 
 def from_behind(block, axis, distance):
@@ -179,7 +188,7 @@
             d_wproj.astype(jnp.bfloat16), "ba", scatter_dimension=1, tiled=True
         ).astype(jnp.float32),
     )
-    half_qkv, half_proj = lax.psum((half_qkv, half_proj), ("ha", "wa"))
+    half_qkv, half_proj = lead_desk_all((half_qkv, half_proj))
     d_table, d_scale, d_gain = lax.psum((d_table, d_scale, d_gain), ("ha", "wa", "ba"))
     return (d_tokens, half_qkv, half_proj, d_table, d_scale, d_gain)
 

time: 218 us -> 226 us (1.037)
  waiting for transfers between devices: 4.03 us -> 25 us
  blocking collectives: 115 us -> 100 us
    reduce_scatter x1, waiting for transfers between devices: 0.01 us -> 21 us  [shards(): lax.psum_scatter(d_wqkv.astype(jnp.bfloat16), 'ba', scatter_dimension=1,...]
    psum x1, blocking collectives: 75.2 us -> 59.6 us  [test_files_on_mesh(): part_next = lax.psum(q_in, across)]
    unnamed x38 -> x42, local copies, waits for them, and re-layouts: 3.95 us -> 5.92 us
  transfers between devices with their start and end apart: 6 -> 7, of which waited for: 2 -> 3; matrix products, arithmetic and copies ran while one was open for 10% -> 9% of each run, Pallas kernels for 0% -> 0%
where the time goes in v1:
time: 226 us; the launch traced here: 222 us
  blocking collectives  100 us (44%)
  matrix products  32.7 us (14%)
  waiting for transfers between devices  25 us (11%)
  local copies, waits for them, and re-layouts  24.7 us (11%)
  other arithmetic  16.8 us (7%)
  between operations  14.5 us (6%)
  starting transfers between devices  8.09 us (4%)
    psum x1, blocking collectives, test_files_on_mesh(): part_next = lax.psum(q_in, across)  59.6 us
    psum x1, blocking collectives, shards(): lax.psum((d_table, d_scale, d_gain), ('ha', 'wa', 'ba'))  40.5 us
    reduce_scatter x1, waiting for transfers between devices, shards(): lax.psum_scatter(d_wqkv.astype(jnp.bfloat16), 'ba', scatter_dimension=1,...  21 us
    dot_general x3, matrix products, fine_product(): return jnp.einsum(form, left, right, precision=HIGHEST)  16.3 us
    ppermute x4, starting transfers between devices, from_behind(): return lax.ppermute(block, axis, route)  7.76 us
    unnamed x42, local copies, waits for them, and re-layouts  5.92 us
    convert_element_type x2, local copies, waits for them, and re-layouts, grads_region(): jnp.stack([d_query, d_key, d_values], 3).astype(jnp.bfloat16)  5.15 us
    dot_general x3, matrix products, coarse_product(): return jnp.einsum(form, left, right, preferred_element_type=jnp.float32)  5.11 us
  transfers between devices with their start and end apart: 7, of which 3 were waited for; matrix products, arithmetic and copies ran while one was open for 9% of the time, Pallas kernels for 0%

profile of v1, /device:TPU:0, one launch (start us, length us, event | category | flops | bytes accessed | tf_op | source)
XLA Modules:
  0.0 221.9 jit_solution(15446519817488703582)
XLA Ops:
  7.2 1.0 pad_maximum_fusion.2
  8.3 4.6 %collective-permute-start = (bf16[2,1,4,32,384]{4,3,2,1,0:T(8,128)(2,1)S(1)}, bf16[2,1,4,32,384]{4,3,2,1,0:T(8,128)(2,1)S(1)}, u32[]{:S(2)}, u32[]{:S(2)}) collective-permute-start(bf16[2,1,4,32,384]{4,3,2,1,0:T(8,128)(2,1)S(1)} %pad_maximum_fusion.2), channel_id=1, source_target_pairs={{4,0},{8,4},{12,8},{16,12},{20,16},{24,20},{28,24},{0,28},{5,1},{9... | collective-permute-start | bytes 589832 | tf_op jit(solution)/shard_map/ppermute | solution.py:27
  12.8 1.1 fusion.52
  14.2 0.8 compare_select_fusion
  15.2 2.0 fusion.2
  17.4 0.9 copy.85
  18.3 1.6 collective-permute-start.1
  20.2 2.8 %collective-permute-done.1 = bf16[2,1,16,4,384]{4,3,2,1,0:T(4,128)(2,1)S(1)} collective-permute-done((bf16[2,1,16,4,384]{4,3,2,1,0:T(4,128)(2,1)S(1)}, bf16[2,1,16,4,384]{4,3,2,1,0:T(4,128)(2,1)S(1)}, u32[]{:S(2)}, u32[]{:S(2)}) %collective-permute-start.1) | collective-permute-done | bytes 98336 | tf_op jit(solution)/shard_map/ppermute | solution.py:27
  23.0 0.9 fusion.57
  24.0 0.7 copy-done.9
  24.7 0.8 convolution_convert_fusion
  25.5 0.6 copy.82
  26.1 3.0 %reshape.449 = bf16[1,8,64,3,12,32]{2,1,5,4,3,0:T(8,128)(2,1)} reshape(bf16[512,1152]{0,1:T(8,128)(2,1)S(1)} %copy.82) | data formatting | bytes 2359296 | tf_op jit(solution)/shard_map/reshape | solution.py:88
  29.2 1.8 fusion.67
  31.7 5.2 %fusion.29 = f32[8,12,64,64]{2,3,1,0:T(8,128)S(1)} fusion(f32[8,64,12]{1,2,0:T(8,128)S(1)} %add_rsqrt_fusion.1, f32[8,64,12]{1,2,0:T(8,128)S(1)} %add_rsqrt_fusion, bf16[1,8,64,1,12,32]{2,1,5,4,3,0:T(8,128)(2,1)S(1)} %get-tuple-element.18, bf16[1,8,64,1,12,32]{2,1,5,4,3,0:T(8,128)(2,1)S(1)} %get-tuple-element.19), kind=kOutput, calls=%fused_computation.41 | convolution fusion | flops 151781376 | bytes 2408448 | tf_op jit(solution)/shard_map/bnqhd,bnkhd->bnhqk/dot_general | solution.py:35
  36.9 1.2 fusion.68
  38.6 0.5 fusion.40
  39.2 1.1 copy-done.3
  40.8 1.3 reshape.451
  42.1 1.6 fusion.69
  43.9 0.9 copy.89
  44.8 2.3 %copy.90 = f32[512,384]{0,1:T(8,128)} copy(f32[512,384]{1,0:T(8,128)} %bitcast.140) | data formatting | bytes 1572864 | tf_op jit(solution)/shard_map/convert_element_type | solution.py:118
  47.1 1.2 fusion.42
  48.3 1.4 multiply_reduce_fusion.2
  49.8 1.4 multiply_convert_fusion
  51.7 1.1 convolution_convert_fusion.5
  53.0 1.3 reshape.452
  54.3 3.6 %multiply_reduce_fusion.1 = (f32[8,12,64]{2,1,0:T(8,128)S(1)}, f32[8,12,64,64]{2,3,1,0:T(8,128)S(1)}) fusion(f32[8,12,64,64]{2,3,1,0:T(8,128)} %copy-done.3, f32[8,12,64]{2,1,0:T(8,128)S(1)} %get-tuple-element.23, bf16[1,8,64,1,12,32]{2,1,5,4,3,0:T(8,128)(2,1)} %copy-done.14, bf16[8,64,12,32]{1,0,3,2:T(8,128)(2,1)} %reshape.452), kind=kOutput, calls=%fused_computation.7 | convolution fusion | flops 26339328 | bytes 3981312 | tf_op jit(solution)/shard_map/bnqhd,bnkhd->bnhqk/dot_general | solution.py:31
  57.9 0.6 copy-done.4
  58.6 2.2 multiply_reduce_fusion
  60.7 4.3 %fusion.22 = (f32[8,64,12]{1,2,0:T(8,128)S(1)}, f32[8,12,32,64]{3,2,1,0:T(8,128)}) fusion(f32[8,64,12]{1,2,0:T(8,128)S(1)} %add_rsqrt_fusion.1, bf16[1,8,64,1,12,32]{2,1,5,4,3,0:T(8,128)(2,1)S(1)} %get-tuple-element.19, f32[8,12,64,64]{2,3,1,0:T(8,128)S(1)} %get-tuple-element.17, f32[12]{0:T(128)S(1)} %minimum_exponential_fusion, ...), kind=kOutput, calls=%fused_computation.35 | convolution fusion | flops 152561664 | bytes 3219504 | tf_op jit(solution)/shard_map/bnhqk,bnkhd->bnqhd/dot_general | solution.py:35
  65.0 6.8 %fusion.18 = (f32[8,64,12]{1,2,0:T(8,128)}, f32[8,12,32,64]{3,2,1,0:T(8,128)}) fusion(f32[8,64,12]{1,2,0:T(8,128)S(1)} %add_rsqrt_fusion, bf16[1,8,64,1,12,32]{2,1,5,4,3,0:T(8,128)(2,1)S(1)} %get-tuple-element.18, f32[8,12,64,64]{2,3,1,0:T(8,128)S(1)} %get-tuple-element.17, f32[12]{0:T(128)S(1)} %minimum_exponential_fusion, ...), kind=kOutput, calls=%fused_computation.31 | convolution fusion | flops 152561664 | bytes 3219504 | tf_op jit(solution)/shard_map/bnhqk,bnqhd->bnkhd/dot_general | solution.py:35
  71.9 0.9 convolution_bitcast_fusion
  73.1 2.6 %fusion.21 = (bf16[1,8,64,1,12,32]{2,5,4,1,3,0:T(8,128)(2,1)S(1)}, bf16[1,8,64,1,12,32]{2,5,4,1,3,0:T(8,128)(2,1)S(1)}) fusion(f32[8,12,32,64]{3,2,1,0:T(8,128)} %get-tuple-element.30, f32[8,64,12]{1,2,0:T(8,128)} %get-tuple-element.29, f32[8,64,12]{1,2,0:T(8,128)S(1)} %add_rsqrt_fusion, bf16[1,8,64,1,12,32]{2,1,5,4,3,0:T(8,128)(2,1)S(1)} %get-tuple-element.18, ...), kind=kLoop, calls=%fused_computation.34 | loop fusion | flops 2359296 | bytes 3244032 | tf_op jit(solution)/shard_map/stack | solution.py:144
  75.7 0.6 maximum_convert_fusion
  76.3 2.7 %copy.98 = bf16[1,8,64,3,12,32]{2,1,5,4,3,0:T(8,128)(2,1)S(1)} copy(bf16[1,8,64,3,12,32]{2,5,4,1,3,0:T(8,128)(2,1)S(1)} %maximum_convert_fusion) | data formatting | bytes 2359296 | tf_op jit(solution)/shard_map/convert_element_type | solution.py:144
  79.1 2.4 %convert_element_type.207 = bf16[512,1152]{0,1:T(8,128)(2,1)} reshape(bf16[1,8,64,3,12,32]{2,1,5,4,3,0:T(8,128)(2,1)S(1)} %copy.98) | data formatting | bytes 2359296 | tf_op jit(solution)/shard_map/convert_element_type | solution.py:144
  81.5 3.1 %convolution_convert_fusion.1 = bf16[384,1152]{0,1:T(8,128)(2,1)} fusion(bf16[512,1152]{0,1:T(8,128)(2,1)} %convert_element_type.207, bf16[512,384]{1,0:T(8,128)(2,1)} %bitcast.142), kind=kOutput, calls=%fused_computation.15 | convolution fusion | flops 453427200 | bytes 2457600 | tf_op jit(solution)/shard_map/dot_general | solution.py:145
  84.6 21.0 %reduce-scatter.3.cloned.1.call-done = bf16[384,576]{0,1:T(8,128)(2,1)} async-done(((bf16[384,1152]{0,1:T(8,128)(2,1)}), bf16[384,576]{0,1:T(8,128)(2,1)}) %reduce-scatter.3.cloned.1.call-update) | async-done | bytes 442384 | tf_op jit(solution)/shard_map/reduce_scatter | solution.py:184
  105.6 59.6 %all-reduce.7 = (f32[384,576]{0,1:T(8,128)}, f32[384,192]{0,1:T(8,128)}) all-reduce(bf16[384,576]{0,1:T(8,128)(2,1)} %reduce-scatter.3.cloned.1.call-done, bf16[384,192]{0,1:T(8,128)(2,1)} %reduce-scatter.5.cloned.1.call-done), channel_id=1, replica_groups=mesh['ha'=8,'wa'=2,'ba'=2] {'ha'}, use_global_device_ids=true, to_apply=%region_12.13 | all-reduce | flops 294912 | bytes 1769472 | tf_op jit(solution)/shard_map/psum | solution.py:17
  165.5 0.9 convolution_convert_fusion.3
  166.5 1.5 collective-permute-start.2
  168.0 1.4 fusion.41
  169.5 1.2 collective-permute-done.2
  170.8 40.5 %all-reduce = (f32[12,225]{1,0:T(8,128)}, f32[12]{0:T(128)}, f32[384]{0:T(512)}) all-reduce(f32[12,225]{1,0:T(8,128)S(1)} %fusion.41, f32[12]{0:T(128)S(1)} %compare_select_fusion.1, f32[384]{0:T(512)S(1)} %get-tuple-element.8), channel_id=1, replica_groups=mesh['ha'=8,'wa'=2,'ba'=2] {'ha','wa','ba'}, use_global_device_ids=true, to_apply=%region_18.19 | all-reduce | flops 3096 | bytes 24768 | tf_op jit(solution)/shard_map/psum | solution.py:192
  211.3 0.9 add_convert_fusion
  212.2 2.2 copy.152
  214.4 0.7 copy.153
  (82 shorter events, 4.4 us)
Async XLA Ops:
  7.2 17.5 %copy-start = (bf16[384,1152]{1,0:T(8,128)(2,1)S(1)}, bf16[384,1152]{1,0:T(8,128)(2,1)}, u32[]{:S(2)}) copy-start(bf16[384,1152]{1,0:T(8,128)(2,1)} %param.9) | copy-start | bytes 2654212
  7.2 8.0 %copy-start.18 = (f32[12,225]{1,0:T(8,128)S(1)}, f32[12,225]{1,0:T(8,128)}, u32[]{:S(2)}) copy-start(f32[12,225]{1,0:T(8,128)} %param.11) | copy-start | bytes 32404
  7.2 77.4 %reduce-scatter.5.cloned.1.call-start = ((), (), s32[]{:S(2)}) async-start(), calls=%async_computation.3 | async-start | bytes 442368 | tf_op jit(solution)/shard_map/reduce_scatter | solution.py:187
  8.3 10.0 %collective-permute-start = (bf16[2,1,4,32,384]{4,3,2,1,0:T(8,128)(2,1)S(1)}, bf16[2,1,4,32,384]{4,3,2,1,0:T(8,128)(2,1)S(1)}, u32[]{:S(2)}, u32[]{:S(2)}) collective-permute-start(bf16[2,1,4,32,384]{4,3,2,1,0:T(8,128)(2,1)S(1)} %pad_maximum_fusion.2), channel_id=1, source_target_pairs={{4,0},{8,4},{12,8},{16,12},{20,16},{24,20},{28,24},{0,28},{5,1},{9... | collective-permute-start | bytes 589832 | tf_op jit(solution)/shard_map/ppermute | solution.py:27
  14.0 4.3 %copy-start.19 = (f32[12]{0:T(128)S(1)}, f32[12]{0:T(128)}, u32[]{:S(2)}) copy-start(f32[12]{0:T(128)} %param.12) | copy-start | bytes 148
  18.3 4.7 %collective-permute-start.1 = (bf16[2,1,16,4,384]{4,3,2,1,0:T(4,128)(2,1)S(1)}, bf16[2,1,16,4,384]{4,3,2,1,0:T(4,128)(2,1)S(1)}, u32[]{:S(2)}, u32[]{:S(2)}) collective-permute-start(bf16[2,1,16,4,384]{4,3,2,1,0:T(4,128)(2,1)S(1)} %pad_maximum_fusion.4), channel_id=1, source_target_pairs={{2,0},{0,2},{3,1},{1,3},{6,4},{4,6},{7,5},{5,7},{10,8},{8,10},{11,... | collective-permute-start | bytes 294920 | tf_op jit(solution)/shard_map/ppermute | solution.py:27
  24.0 0.7 copy-start.9
  30.9 7.7 %copy-start.14 = (bf16[1,8,64,1,12,32]{2,1,5,4,3,0:T(8,128)(2,1)}, bf16[1,8,64,1,12,32]{2,1,5,4,3,0:T(8,128)(2,1)S(1)}, u32[]{:S(2)}) copy-start(bf16[1,8,64,1,12,32]{2,1,5,4,3,0:T(8,128)(2,1)S(1)} %get-tuple-element.20) | copy-start | bytes 1179652
  31.7 5.2 %copy-start.10 = (f32[12,64,64]{1,2,0:T(8,128)S(1)}, f32[12,64,64]{1,2,0:T(8,128)}, u32[]{:S(2)}) copy-start(f32[12,64,64]{1,2,0:T(8,128)} %copy.85) | copy-start | bytes 589828
  31.7 5.2 %copy-start.13 = (f32[8,64,64]{1,2,0:T(8,128)S(1)}, f32[8,64,64]{1,2,0:T(8,128)}, u32[]{:S(2)}) copy-start(f32[8,64,64]{1,2,0:T(8,128)} %compare_select_fusion) | copy-start | bytes 393220
  36.9 1.7 copy-start.1
  38.6 1.7 copy-start.3
  42.1 1.7 copy-start.6
  43.9 3.2 %copy-start.17 = (f32[384]{0:T(512)S(1)}, f32[384]{0:T(512)}, u32[]{:S(2)}) copy-start(f32[384]{0:T(512)} %param.13) | copy-start | bytes 4612
  49.8 1.4 copy-start.12
  49.8 1.9 copy-start.5
  54.3 3.6 %copy-start.2 = (f32[8,12,64,64]{2,3,1,0:T(8,128)S(1)}, f32[8,12,64,64]{2,3,1,0:T(8,128)}, u32[]{:S(2)}) copy-start(f32[8,12,64,64]{2,3,1,0:T(8,128)} %copy-done.1) | copy-start | bytes 4718596
  54.3 4.3 %copy-start.4 = (f32[8,12,64,64]{2,3,1,0:T(8,128)S(1)}, f32[8,12,64,64]{2,3,1,0:T(8,128)}, u32[]{:S(2)}) copy-start(f32[8,12,64,64]{2,3,1,0:T(8,128)} %copy-done.3) | copy-start | bytes 4718596
  65.0 6.8 %copy-start.15 = (bf16[8,64,12,32]{1,0,3,2:T(8,128)(2,1)S(1)}, bf16[8,64,12,32]{1,0,3,2:T(8,128)(2,1)}, u32[]{:S(2)}) copy-start(bf16[8,64,12,32]{1,0,3,2:T(8,128)(2,1)} %reshape.452) | copy-start | bytes 1179652
  72.8 32.7 %reduce-scatter.3.cloned.1.call-start = ((), (), s32[]{:S(2)}) async-start(), calls=%async_computation.2 | async-start | bytes 1327104 | tf_op jit(solution)/shard_map/reduce_scatter | solution.py:184
  84.5 80.7 %copy-start.8 = (f32[12,64,64]{1,2,0:T(8,128)S(1)}, f32[12,64,64]{1,2,0:T(8,128)}, u32[]{:S(2)}) copy-start(f32[12,64,64]{1,2,0:T(8,128)} %get-tuple-element.7) | copy-start | bytes 589828
  84.5 81.0 %copy-start.11 = (bf16[512,1152]{0,1:T(8,128)(2,1)S(1)}, bf16[512,1152]{0,1:T(8,128)(2,1)}, u32[]{:S(2)}) copy-start(bf16[512,1152]{0,1:T(8,128)(2,1)} %convert_element_type.207) | copy-start | bytes 3538948
  84.6 127.6 %all-reduce.6.cloned.1.call-start = ((), (), s32[]{:S(2)}) async-start(), calls=%async_computation.4 | async-start | bytes 2359296 | tf_op jit(solution)/shard_map/psum | solution.py:18
  166.4 44.9 %copy-start.7 = (bf16[1,16,32,384]{3,2,1,0:T(8,128)(2,1)S(1)}, bf16[1,16,32,384]{3,2,1,0:T(8,128)(2,1)}, u32[]{:S(2)}) copy-start(bf16[1,16,32,384]{3,2,1,0:T(8,128)(2,1)} %param.8) | copy-start | bytes 1179652
  166.5 4.2 %collective-permute-start.2 = (bf16[1,16,4,384]{3,2,1,0:T(4,128)(2,1)S(1)}, bf16[1,16,4,384]{3,2,1,0:T(4,128)(2,1)S(1)}, u32[]{:S(2)}, u32[]{:S(2)}) collective-permute-start(bf16[1,16,4,384]{3,2,1,0:T(4,128)(2,1)S(1)} %slice.61), channel_id=1, source_target_pairs={{2,0},{0,2},{3,1},{1,3},{6,4},{4,6},{7,5},{5,7},{10,8},{8,10},{11,... | collective-permute-start | bytes 147464 | tf_op jit(solution)/shard_map/ppermute | solution.py:27
  170.7 40.6 %collective-permute-start.3 = (bf16[1,4,32,384]{3,2,1,0:T(8,128)(2,1)S(1)}, bf16[1,4,32,384]{3,2,1,0:T(8,128)(2,1)S(1)}, u32[]{:S(2)}, u32[]{:S(2)}) collective-permute-start(bf16[1,4,32,384]{3,2,1,0:T(8,128)(2,1)S(1)} %pad_maximum_fusion.3), channel_id=1, source_target_pairs={{28,0},{0,4},{4,8},{8,12},{12,16},{16,20},{20,24},{24,28},{29,1},{... | collective-permute-start | bytes 294920 | tf_op jit(solution)/shard_map/ppermute | solution.py:27
  212.2 2.2 copy-start.16
Sparse Core Ops, SparseCore 0:
  73.0 11.1 reduce-scatter.4
  87.0 18.5 reduce-scatter.2
  165.3 41.9 all-reduce.5
